TPU v7x, 32 devices: a whole 2x2x4 slice. The times are simulated.
32 devices in a mesh: gx: 4 (over y, x), gy: 8 (over z, core).
Axes of the slice: x: 2, y: 2, z: 4, core: 2. Of those that a mesh axis runs over, the one named last changes fastest.
Arguments:
- right_side: float32 [128, 2048], P('gx', 'gy'), may hold values from -200 to 200
- reaction: float32 [128, 2048], P('gx', 'gy'), may hold values from 2 to 4
- kernel: float32 [65, 65], replicated, may hold values from -0.04 to 0.04
Outputs:
- solution: float32 [128, 2048], P('gx', 'gy')
- residual: float32 [128, 2048], P('gx', 'gy')
All inputs are finite; a program needn't handle non-finite values.
Results may differ from a plain program's by a relative error of at most 0.00075.
Values sent between devices are 32-bit elements; how exact they have to be, the bound alone decides.
A program may use at most 64 MiB of HBM per device.

v0:
```python
import jax
import jax.numpy as jnp
from jax import lax
from jax.sharding import PartitionSpec as P

ITERS = 4
small_term = 1e-06


def extended(block, sides, width):
    for axis, dim in sides:
        count = lax.axis_size(axis)
        forward = [(i, i + 1) for i in range(count - 1)]
        backward = [(target, source) for source, target in forward]
        low = lax.ppermute(
            lax.slice_in_dim(block, block.shape[dim] - width, None, axis=dim), axis, forward
        )
        high = lax.ppermute(lax.slice_in_dim(block, 0, width, axis=dim), axis, backward)
        block = jnp.concatenate([low, block, high], axis=dim)
    return block


def solve_small(normal_matrix, target, count):
    factor = jnp.linalg.cholesky(normal_matrix)
    forward = []
    for position in range(count):
        accum = target[position]
        for earlier in range(position):
            accum = accum - factor[position, earlier] * forward[earlier]
        forward.append(accum / factor[position, position])
    backward = [None] * count
    for position in reversed(range(count)):
        accum = forward[position]
        for later in range(position + 1, count):
            accum = accum - factor[later, position] * backward[later]
        backward[position] = accum / factor[position, position]
    return backward


def total_norm(values):
    return jnp.sqrt(lax.psum(jnp.sum(values * values), ("gx", "gy")) + small_term)


def local(right_side, reaction, kernel):
    tile_rows, tile_cols = right_side.shape
    kernel_width = kernel.shape[0]
    radius = kernel_width // 2
    bundle = 5
    span_rows = tile_rows + 2 * radius
    period = 2 * tile_rows + 2 * radius
    highest = lax.Precision.HIGHEST

    def extend(values):
        return extended(values, (("gx", 0), ("gy", 1)), radius)

    def apply_operator(values):
        padded = extend(values)

        def group_step(group, summed):
            first_col = group * bundle
            chosen = lax.dynamic_slice_in_dim(kernel, first_col, bundle, 1)
            columns_rev = jnp.pad(chosen[::-1, :].T, ((0, 0), (0, period - kernel_width)))
            toeplitz = jnp.tile(columns_rev, (1, tile_rows))[:, : tile_rows * (period - 1)]
            toeplitz = toeplitz.reshape(bundle, tile_rows, period - 1)[:, :, :span_rows]
            for member in range(bundle):
                offset = 2 * radius - first_col - member
                shifted = lax.dynamic_slice_in_dim(padded, offset, tile_cols, 1)
                summed = summed + jnp.dot(
                    toeplitz[member], shifted, precision=highest, preferred_element_type=jnp.float32
                )
            return summed

        convolved = lax.fori_loop(
            0, kernel_width // bundle, group_step, jnp.zeros((tile_rows, tile_cols), jnp.float32)
        )
        return reaction * values - convolved

    initial_norm = total_norm(right_side)
    krylov = [right_side / initial_norm]
    upper = jnp.zeros((ITERS + 1, ITERS), jnp.float32)
    for column in range(ITERS):
        candidate = apply_operator(krylov[column])
        basis_now = jnp.stack(krylov)
        first_terms = jnp.einsum("kij,ij->k", basis_now, candidate, precision=highest)
        first_terms = lax.psum(first_terms, ("gx", "gy"))
        candidate = candidate - jnp.einsum("k,kij->ij", first_terms, basis_now, precision=highest)
        upper = upper.at[: column + 1, column].set(first_terms)
        length = total_norm(candidate)
        upper = upper.at[column + 1, column].set(length)
        krylov.append(candidate / length)
    normal_matrix = jnp.dot(upper.T, upper, precision=highest)
    coeffs = solve_small(normal_matrix, initial_norm * upper[0, :], ITERS)
    solution = coeffs[0] * krylov[0]
    for column in range(1, ITERS):
        solution = solution + coeffs[column] * krylov[column]
    residual = right_side - apply_operator(solution)
    return (solution, residual)


def solution(mesh):
    in_specs = (P("gx", "gy"), P("gx", "gy"), P())
    out_specs = (P("gx", "gy"), P("gx", "gy"))
    return jax.shard_map(local, mesh=mesh, in_specs=in_specs, out_specs=out_specs, check_vma=False)
```

profile of v0, /device:TPU:3, one launch (start us, length us, event | category | flops | bytes accessed | tf_op | source)
XLA Modules:
  0.0 615.0 jit_solution(7024932952548193070)
XLA Ops:
  2.1 39.9 %psum.63 = f32[]{:T(128)} all-reduce(f32[]{:T(128)} %multiply_reduce_fusion.4), channel_id=1, replica_groups=mesh['gx'=4,'gy'=8] {'gx','gy'}, use_global_device_ids=true, to_apply=%region_1.0 | all-reduce | flops 1 | bytes 8 | tf_op jit(solution)/shard_map/psum | solution.py:41
  51.5 6.8 %collective-permute-start.2 = (f32[96,32]{1,0:T(8,128)S(1)}, f32[96,32]{1,0:T(8,128)S(1)}, u32[]{:S(2)}, u32[]{:S(2)}) collective-permute-start(f32[96,32]{1,0:T(8,128)S(1)} %get-tuple-element.973), channel_id=1, source_target_pairs={{0,1},{1,2},{2,3},{3,4},{4,5},{5,6},{6,7},{8,9},{9,10},{10,11},{11... | collective-permute-start | bytes 36872 | tf_op jit(solution)/shard_map/ppermute | solution.py:15
  63.9 24.5 %while.98 = (s32[]{:T(128)}, f32[32,256]{1,0:T(8,128)S(1)}, f32[65,65]{1,0:T(8,128)S(1)}, f32[96,320]{1,0:T(8,128)S(1)}, s32[]{:T(128)}, /*index=5*/s32[]{:T(128...) while((s32[]{:T(128)}, f32[32,256]{1,0:T(8,128)S(1)}, ...), condition=%wide.region_3.4_spmd.clone, body=%wide.region_2.3_spmd.clone.sunk | while | flops 47235088 | bytes 1324147 | solution.py:73
  89.1 38.0 %psum.64 = f32[1]{0:T(128)} all-reduce(f32[1]{0:T(128)} %bitcast), channel_id=1, replica_groups=mesh['gx'=4,'gy'=8] {'gx','gy'}, use_global_device_ids=true, to_apply=%region_4.5 | all-reduce | flops 1 | bytes 8 | tf_op jit(solution)/shard_map/psum | solution.py:85
  128.4 40.4 %psum.65 = f32[]{:T(128)} all-reduce(f32[]{:T(128)} %get-tuple-element.963), channel_id=1, replica_groups=mesh['gx'=4,'gy'=8] {'gx','gy'}, use_global_device_ids=true, to_apply=%region_6.7 | all-reduce | flops 1 | bytes 8 | tf_op jit(solution)/shard_map/psum | solution.py:41
  174.8 3.3 collective-permute-done.5
  178.2 6.0 collective-permute-start.6
  186.1 3.5 collective-permute-done.7
  189.7 24.5 %while.99 = (s32[]{:T(128)}, f32[32,256]{1,0:T(8,128)S(1)}, f32[65,65]{1,0:T(8,128)S(1)}, f32[96,320]{1,0:T(8,128)S(1)}, s32[]{:T(128)}, /*index=5*/s32[]{:T(128...) while((s32[]{:T(128)}, f32[32,256]{1,0:T(8,128)S(1)}, ...), condition=%wide.region_9.10_spmd.clone, body=%wide.region_8.9_spmd.clone.sunk | while | flops 47235088 | bytes 1324147 | solution.py:73
  215.5 37.4 %psum.66 = f32[2]{0:T(128)S(1)} all-reduce(f32[2]{0:T(128)S(1)} %convolution_bitcast_fusion.2), channel_id=1, replica_groups=mesh['gx'=4,'gy'=8] {'gx','gy'}, use_global_device_ids=true, to_apply=%region_10.11 | all-reduce | flops 2 | bytes 16 | tf_op jit(solution)/shard_map/psum | solution.py:85
  254.0 40.5 %psum.67 = f32[]{:T(128)} all-reduce(f32[]{:T(128)} %multiply_reduce_fusion.2), channel_id=1, replica_groups=mesh['gx'=4,'gy'=8] {'gx','gy'}, use_global_device_ids=true, to_apply=%region_12.13 | all-reduce | flops 1 | bytes 8 | tf_op jit(solution)/shard_map/psum | solution.py:41
  304.0 5.8 collective-permute-start.10
  311.7 3.5 collective-permute-done.11
  315.3 24.5 %while.100 = (s32[]{:T(128)}, f32[32,256]{1,0:T(8,128)S(1)}, f32[65,65]{1,0:T(8,128)S(1)}, f32[96,320]{1,0:T(8,128)S(1)}, s32[]{:T(128)}, /*index=5*/s32[]{:T(12...) while((s32[]{:T(128)}, f32[32,256]{1,0:T(8,128)S(1)}, ...), condition=%wide.region_15.16_spmd.clone, body=%wide.region_14.15_spmd.clone.sunk | while | flops 47235088 | bytes 1324147 | solution.py:73
  341.9 37.4 %psum.68 = f32[3]{0:T(128)S(1)} all-reduce(f32[3]{0:T(128)S(1)} %convolution_bitcast_fusion.1), channel_id=1, replica_groups=mesh['gx'=4,'gy'=8] {'gx','gy'}, use_global_device_ids=true, to_apply=%region_16.17 | all-reduce | flops 3 | bytes 24 | tf_op jit(solution)/shard_map/psum | solution.py:85
  380.4 40.5 %psum.69 = f32[]{:T(128)} all-reduce(f32[]{:T(128)} %multiply_reduce_fusion.1), channel_id=1, replica_groups=mesh['gx'=4,'gy'=8] {'gx','gy'}, use_global_device_ids=true, to_apply=%region_18.19 | all-reduce | flops 1 | bytes 8 | tf_op jit(solution)/shard_map/psum | solution.py:41
  430.4 5.8 collective-permute-start.14
  441.7 24.5 %while.101 = (s32[]{:T(128)}, f32[32,256]{1,0:T(8,128)S(1)}, f32[65,65]{1,0:T(8,128)S(1)}, f32[96,320]{1,0:T(8,128)S(1)}, s32[]{:T(128)}, /*index=5*/s32[]{:T(12...) while((s32[]{:T(128)}, f32[32,256]{1,0:T(8,128)S(1)}, ...), condition=%wide.region_21.22_spmd.clone, body=%wide.region_20.21_spmd.clone.sunk | while | flops 47235088 | bytes 1324147 | solution.py:73
  468.2 37.4 %psum.70 = f32[4]{0:T(128)S(1)} all-reduce(f32[4]{0:T(128)S(1)} %convolution_bitcast_fusion), channel_id=1, replica_groups=mesh['gx'=4,'gy'=8] {'gx','gy'}, use_global_device_ids=true, to_apply=%region_22.23 | all-reduce | flops 4 | bytes 32 | tf_op jit(solution)/shard_map/psum | solution.py:85
  506.8 40.5 %psum.71 = f32[]{:T(128)} all-reduce(f32[]{:T(128)} %fusion.60), channel_id=1, replica_groups=mesh['gx'=4,'gy'=8] {'gx','gy'}, use_global_device_ids=true, to_apply=%region_24.25 | all-reduce | flops 1 | bytes 8 | tf_op jit(solution)/shard_map/psum | solution.py:41
  575.1 3.4 collective-permute-done.17
  578.6 5.8 collective-permute-start.18
  586.3 3.5 collective-permute-done.19
  589.9 24.5 %while.102 = (s32[]{:T(128)}, f32[32,256]{1,0:T(8,128)S(1)}, f32[65,65]{1,0:T(8,128)S(1)}, f32[96,320]{1,0:T(8,128)S(1)}, s32[]{:T(128)}, /*index=5*/s32[]{:T(12...) while((s32[]{:T(128)}, f32[32,256]{1,0:T(8,128)S(1)}, ...), condition=%wide.region_28.29_spmd.clone, body=%wide.region_27.28_spmd.clone.sunk | while | flops 47235088 | bytes 1324147 | solution.py:73
  (898 shorter events, 187.0 us)
Async XLA Ops:
  0.6 42.1 %copy-start.1 = (f32[32,256]{1,0:T(8,128)S(1)}, f32[32,256]{1,0:T(8,128)}, u32[]{:S(2)}) copy-start(f32[32,256]{1,0:T(8,128)} %param.29) | copy-start | bytes 98308
  42.7 7.9 %collective-permute-start = (f32[32,256]{1,0:T(8,128)S(1)}, f32[32,256]{1,0:T(8,128)S(1)}, u32[]{:S(2)}, u32[]{:S(2)}) collective-permute-start(f32[32,256]{1,0:T(8,128)S(1)} %broadcast_divide_fusion.3), channel_id=1, source_target_pairs={{0,8},{8,16},{16,24},{1,9},{9,17},{17,25},{2,10},{10,18},{18,26},{... | collective-permute-start | bytes 98312 | tf_op jit(solution)/shard_map/ppermute | solution.py:15
  45.8 5.6 collective-permute-start.1
  51.5 10.1 %collective-permute-start.2 = (f32[96,32]{1,0:T(8,128)S(1)}, f32[96,32]{1,0:T(8,128)S(1)}, u32[]{:S(2)}, u32[]{:S(2)}) collective-permute-start(f32[96,32]{1,0:T(8,128)S(1)} %get-tuple-element.973), channel_id=1, source_target_pairs={{0,1},{1,2},{2,3},{3,4},{4,5},{5,6},{6,7},{8,9},{9,10},{10,11},{11... | collective-permute-start | bytes 36872 | tf_op jit(solution)/shard_map/ppermute | solution.py:15
  58.3 5.4 collective-permute-start.3
  61.6 2.3 copy-start
  63.9 24.5 %copy-start.2 = (f32[32,256]{1,0:T(8,128)S(1)}, f32[32,256]{1,0:T(8,128)}, u32[]{:S(2)}) copy-start(f32[32,256]{1,0:T(8,128)} %param.30) | copy-start | bytes 98308
  169.4 5.3 collective-permute-start.4
  172.5 5.6 collective-permute-start.5
  178.2 7.9 %collective-permute-start.6 = (f32[96,32]{1,0:T(8,128)S(1)}, f32[96,32]{1,0:T(8,128)S(1)}, u32[]{:S(2)}, u32[]{:S(2)}) collective-permute-start(f32[96,32]{1,0:T(8,128)S(1)} %get-tuple-element.971), channel_id=1, source_target_pairs={{0,1},{1,2},{2,3},{3,4},{4,5},{5,6},{6,7},{8,9},{9,10},{10,11},{11... | collective-permute-start | bytes 36872 | tf_op jit(solution)/shard_map/ppermute | solution.py:15
  184.1 5.4 collective-permute-start.7
  295.2 7.2 %collective-permute-start.8 = (f32[32,256]{1,0:T(8,128)S(1)}, f32[32,256]{1,0:T(8,128)S(1)}, u32[]{:S(2)}, u32[]{:S(2)}) collective-permute-start(f32[32,256]{1,0:T(8,128)S(1)} %broadcast_divide_fusion.1), channel_id=1, source_target_pairs={{0,8},{8,16},{16,24},{1,9},{9,17},{17,25},{2,10},{10,18},{18,26},{... | collective-permute-start | bytes 98312 | tf_op jit(solution)/shard_map/ppermute | solution.py:15
  298.3 5.6 collective-permute-start.9
  304.0 7.7 %collective-permute-start.10 = (f32[96,32]{1,0:T(8,128)S(1)}, f32[96,32]{1,0:T(8,128)S(1)}, u32[]{:S(2)}, u32[]{:S(2)}) collective-permute-start(f32[96,32]{1,0:T(8,128)S(1)} %get-tuple-element.969), channel_id=1, source_target_pairs={{0,1},{1,2},{2,3},{3,4},{4,5},{5,6},{6,7},{8,9},{9,10},{10,11},{11... | collective-permute-start | bytes 36872 | tf_op jit(solution)/shard_map/ppermute | solution.py:15
  309.8 5.4 collective-permute-start.11
  421.7 7.1 %collective-permute-start.12 = (f32[32,256]{1,0:T(8,128)S(1)}, f32[32,256]{1,0:T(8,128)S(1)}, u32[]{:S(2)}, u32[]{:S(2)}) collective-permute-start(f32[32,256]{1,0:T(8,128)S(1)} %broadcast_divide_fusion), channel_id=1, source_target_pairs={{0,8},{8,16},{16,24},{1,9},{9,17},{17,25},{2,10},{10,18},{18,26},{... | collective-permute-start | bytes 98312 | tf_op jit(solution)/shard_map/ppermute | solution.py:15
  424.8 5.6 collective-permute-start.13
  430.4 7.9 %collective-permute-start.14 = (f32[96,32]{1,0:T(8,128)S(1)}, f32[96,32]{1,0:T(8,128)S(1)}, u32[]{:S(2)}, u32[]{:S(2)}) collective-permute-start(f32[96,32]{1,0:T(8,128)S(1)} %get-tuple-element.967), channel_id=1, source_target_pairs={{0,1},{1,2},{2,3},{3,4},{4,5},{5,6},{6,7},{8,9},{9,10},{10,11},{11... | collective-permute-start | bytes 36872 | tf_op jit(solution)/shard_map/ppermute | solution.py:15
  436.2 5.4 collective-permute-start.15
  569.8 44.5 %copy-start.3 = (f32[32,256]{1,0:T(8,128)}, f32[32,256]{1,0:T(8,128)S(1)}, u32[]{:S(2)}) copy-start(f32[32,256]{1,0:T(8,128)S(1)} %multiply_add_fusion) | copy-start | bytes 98308
  569.8 5.3 collective-permute-start.16
  572.9 5.6 collective-permute-start.17
  578.6 7.7 %collective-permute-start.18 = (f32[96,32]{1,0:T(8,128)S(1)}, f32[96,32]{1,0:T(8,128)S(1)}, u32[]{:S(2)}, u32[]{:S(2)}) collective-permute-start(f32[96,32]{1,0:T(8,128)S(1)} %get-tuple-element.965), channel_id=1, source_target_pairs={{0,1},{1,2},{2,3},{3,4},{4,5},{5,6},{6,7},{8,9},{9,10},{10,11},{11... | collective-permute-start | bytes 36872 | tf_op jit(solution)/shard_map/ppermute | solution.py:15
  584.4 5.4 collective-permute-start.19
  (2 other events, 1.3 us)
where the time goes:
time: 618 us; the launch traced here: 615 us
  blocking collectives  352 us (57%)
  matrix products  87.7 us (14%)
  starting transfers between devices  66.3 us (11%)
  local copies, waits for them, and re-layouts  37.8 us (6%)
  waiting for transfers between devices  26.2 us (4%)
  between operations  19.8 us (3%)
  other arithmetic  16.1 us (3%)
  loops' own time  8.91 us (1%)
    psum x5, blocking collectives, total_norm(): lax.psum(jnp.sum(values * values), ('gx', 'gy')) + small_term  202 us
    psum x4, blocking collectives, local(): first_terms = lax.psum(first_terms, ('gx', 'gy'))  150 us
    dot_general x325, matrix products, group_step(): jnp.dot(toeplitz[member], shifted, precision=highest, preferred_element_t...  84.5 us
    ppermute x10, starting transfers between devices, extended(): lax.ppermute(lax.slice_in_dim(block, block.shape[dim] - width, None, axis...  45.6 us
    ppermute x10, waiting for transfers between devices, extended(): lax.ppermute(lax.slice_in_dim(block, 0, width, axis=dim), axis, backward)  26.2 us
    ppermute x10, starting transfers between devices, extended(): lax.ppermute(lax.slice_in_dim(block, 0, width, axis=dim), axis, backward)  20.7 us
    reshape x65, local copies, waits for them, and re-layouts, group_step(): toeplitz = toeplitz.reshape(bundle, tile_rows, period - 1)[:, :, :span_rows]  12.6 us
  transfers between devices with their start and end apart: 20, of which 10 were waited for; matrix products, arithmetic and copies ran while one was open for 1% of the time, Pallas kernels for 0%

commit v1 on v0

--- a/solution.py
+++ b/solution.py
@@ -82,7 +82,8 @@
         candidate = apply_operator(krylov[column])
         basis_now = jnp.stack(krylov)
         first_terms = jnp.einsum("kij,ij->k", basis_now, candidate, precision=highest)
-        first_terms = lax.psum(first_terms, ("gx", "gy"))
+        for name in ("gy", "gx"):
+            first_terms = lax.psum(first_terms, name)
         candidate = candidate - jnp.einsum("k,kij->ij", first_terms, basis_now, precision=highest)
         upper = upper.at[: column + 1, column].set(first_terms)
         length = total_norm(candidate)

time: 618 us -> 552 us (0.89)
  blocking collectives: 352 us -> 280 us
    psum x4 -> x8, blocking collectives: 150 us -> 66.7 us  [local(): first_terms = lax.psum(first_terms, name)]
    psum x5, blocking collectives: 202 us -> 213 us  [total_norm(): lax.psum(jnp.sum(values * values), ('gx', 'gy')) + small_term]
  transfers between devices with their start and end apart: 20 -> 20, of which waited for: 10 -> 9; matrix products, arithmetic and copies ran while one was open for 1% -> 1% of each run, Pallas kernels for 0% -> 0%
where the time goes in v1:
time: 552 us; the launch traced here: 550 us
  blocking collectives  280 us (51%)
  matrix products  87.7 us (16%)
  starting transfers between devices  71.9 us (13%)
  local copies, waits for them, and re-layouts  37.8 us (7%)
  waiting for transfers between devices  28.1 us (5%)
  between operations  19.9 us (4%)
  other arithmetic  16 us (3%)
  loops' own time  8.9 us (2%)
    psum x5, blocking collectives, total_norm(): lax.psum(jnp.sum(values * values), ('gx', 'gy')) + small_term  213 us
    dot_general x325, matrix products, group_step(): jnp.dot(toeplitz[member], shifted, precision=highest, preferred_element_t...  84.5 us
    psum x8, blocking collectives, local(): first_terms = lax.psum(first_terms, name)  66.7 us
    ppermute x10, starting transfers between devices, extended(): lax.ppermute(lax.slice_in_dim(block, block.shape[dim] - width, None, axis...  51.4 us
    ppermute x10, waiting for transfers between devices, extended(): lax.ppermute(lax.slice_in_dim(block, 0, width, axis=dim), axis, backward)  28.1 us
    ppermute x10, starting transfers between devices, extended(): lax.ppermute(lax.slice_in_dim(block, 0, width, axis=dim), axis, backward)  20.5 us
    reshape x65, local copies, waits for them, and re-layouts, group_step(): toeplitz = toeplitz.reshape(bundle, tile_rows, period - 1)[:, :, :span_rows]  12.6 us
  transfers between devices with their start and end apart: 20, of which 9 were waited for; matrix products, arithmetic and copies ran while one was open for 1% of the time, Pallas kernels for 0%

profile of v1, /device:TPU:3, one launch (start us, length us, event | category | flops | bytes accessed | tf_op | source)
XLA Modules:
  0.0 550.2 jit_solution(3730955331381555176)
XLA Ops:
  2.1 39.9 %psum.91 = f32[]{:T(128)} all-reduce(f32[]{:T(128)} %multiply_reduce_fusion.4), channel_id=1, replica_groups=mesh['gx'=4,'gy'=8] {'gx','gy'}, use_global_device_ids=true, to_apply=%region_1.0 | all-reduce | flops 1 | bytes 8 | tf_op jit(solution)/shard_map/psum | solution.py:41
  51.5 6.8 %collective-permute-start.2 = (f32[96,32]{1,0:T(8,128)S(1)}, f32[96,32]{1,0:T(8,128)S(1)}, u32[]{:S(2)}, u32[]{:S(2)}) collective-permute-start(f32[96,32]{1,0:T(8,128)S(1)} %get-tuple-element.973), channel_id=1, source_target_pairs={{0,1},{1,2},{2,3},{3,4},{4,5},{5,6},{6,7},{8,9},{9,10},{10,11},{11... | collective-permute-start | bytes 36872 | tf_op jit(solution)/shard_map/ppermute | solution.py:15
  63.9 24.5 %while.98 = (s32[]{:T(128)}, f32[32,256]{1,0:T(8,128)S(1)}, f32[65,65]{1,0:T(8,128)S(1)}, f32[96,320]{1,0:T(8,128)S(1)}, s32[]{:T(128)}, /*index=5*/s32[]{:T(128...) while((s32[]{:T(128)}, f32[32,256]{1,0:T(8,128)S(1)}, ...), condition=%wide.region_3.4_spmd.clone, body=%wide.region_2.3_spmd.clone.sunk | while | flops 47235088 | bytes 1324147 | solution.py:73
  89.0 11.3 %psum.92 = f32[1]{0:T(128)} all-reduce(f32[1]{0:T(128)} %bitcast), channel_id=1, replica_groups=mesh['gx'=4,'gy'=8] {'gy'}, use_global_device_ids=true, to_apply=%region_4.5 | all-reduce | flops 1 | bytes 8 | tf_op jit(solution)/shard_map/psum | solution.py:86
  100.3 6.1 %psum.93 = f32[1]{0:T(128)} all-reduce(f32[1]{0:T(128)} %psum.92), channel_id=1, replica_groups=mesh['gx'=4,'gy'=8] {'gx'}, use_global_device_ids=true, to_apply=%region_5.6 | all-reduce | flops 1 | bytes 8 | tf_op jit(solution)/shard_map/psum | solution.py:86
  107.7 43.5 %psum.94 = f32[]{:T(128)} all-reduce(f32[]{:T(128)} %get-tuple-element.963), channel_id=1, replica_groups=mesh['gx'=4,'gy'=8] {'gx','gy'}, use_global_device_ids=true, to_apply=%region_7.8 | all-reduce | flops 1 | bytes 8 | tf_op jit(solution)/shard_map/psum | solution.py:41
  160.7 7.3 %collective-permute-start.6 = (f32[96,32]{1,0:T(8,128)S(1)}, f32[96,32]{1,0:T(8,128)S(1)}, u32[]{:S(2)}, u32[]{:S(2)}) collective-permute-start(f32[96,32]{1,0:T(8,128)S(1)} %get-tuple-element.971), channel_id=1, source_target_pairs={{0,1},{1,2},{2,3},{3,4},{4,5},{5,6},{6,7},{8,9},{9,10},{10,11},{11... | collective-permute-start | bytes 36872 | tf_op jit(solution)/shard_map/ppermute | solution.py:15
  173.5 24.5 %while.99 = (s32[]{:T(128)}, f32[32,256]{1,0:T(8,128)S(1)}, f32[65,65]{1,0:T(8,128)S(1)}, f32[96,320]{1,0:T(8,128)S(1)}, s32[]{:T(128)}, /*index=5*/s32[]{:T(128...) while((s32[]{:T(128)}, f32[32,256]{1,0:T(8,128)S(1)}, ...), condition=%wide.region_10.11_spmd.clone, body=%wide.region_9.10_spmd.clone.sunk | while | flops 47235088 | bytes 1324147 | solution.py:73
  198.6 10.7 %psum.95 = f32[2]{0:T(128)S(1)} all-reduce(f32[2]{0:T(128)S(1)} %convolution_bitcast_fusion.2), channel_id=1, replica_groups=mesh['gx'=4,'gy'=8] {'gy'}, use_global_device_ids=true, to_apply=%region_11.12 | all-reduce | flops 2 | bytes 16 | tf_op jit(solution)/shard_map/psum | solution.py:86
  210.0 5.5 psum.96
  216.4 43.4 %psum.97 = f32[]{:T(128)} all-reduce(f32[]{:T(128)} %multiply_reduce_fusion.2), channel_id=1, replica_groups=mesh['gx'=4,'gy'=8] {'gx','gy'}, use_global_device_ids=true, to_apply=%region_14.15 | all-reduce | flops 1 | bytes 8 | tf_op jit(solution)/shard_map/psum | solution.py:41
  269.3 7.3 %collective-permute-start.10 = (f32[96,32]{1,0:T(8,128)S(1)}, f32[96,32]{1,0:T(8,128)S(1)}, u32[]{:S(2)}, u32[]{:S(2)}) collective-permute-start(f32[96,32]{1,0:T(8,128)S(1)} %get-tuple-element.969), channel_id=1, source_target_pairs={{0,1},{1,2},{2,3},{3,4},{4,5},{5,6},{6,7},{8,9},{9,10},{10,11},{11... | collective-permute-start | bytes 36872 | tf_op jit(solution)/shard_map/ppermute | solution.py:15
  282.1 24.5 %while.100 = (s32[]{:T(128)}, f32[32,256]{1,0:T(8,128)S(1)}, f32[65,65]{1,0:T(8,128)S(1)}, f32[96,320]{1,0:T(8,128)S(1)}, s32[]{:T(128)}, /*index=5*/s32[]{:T(12...) while((s32[]{:T(128)}, f32[32,256]{1,0:T(8,128)S(1)}, ...), condition=%wide.region_17.18_spmd.clone, body=%wide.region_16.17_spmd.clone.sunk | while | flops 47235088 | bytes 1324147 | solution.py:73
  307.9 10.7 %psum.98 = f32[3]{0:T(128)S(1)} all-reduce(f32[3]{0:T(128)S(1)} %convolution_bitcast_fusion.1), channel_id=1, replica_groups=mesh['gx'=4,'gy'=8] {'gy'}, use_global_device_ids=true, to_apply=%region_18.19 | all-reduce | flops 3 | bytes 24 | tf_op jit(solution)/shard_map/psum | solution.py:86
  319.2 5.5 psum.99
  325.8 43.5 %psum.100 = f32[]{:T(128)} all-reduce(f32[]{:T(128)} %multiply_reduce_fusion.1), channel_id=1, replica_groups=mesh['gx'=4,'gy'=8] {'gx','gy'}, use_global_device_ids=true, to_apply=%region_21.22 | all-reduce | flops 1 | bytes 8 | tf_op jit(solution)/shard_map/psum | solution.py:41
  378.9 7.1 %collective-permute-start.14 = (f32[96,32]{1,0:T(8,128)S(1)}, f32[96,32]{1,0:T(8,128)S(1)}, u32[]{:S(2)}, u32[]{:S(2)}) collective-permute-start(f32[96,32]{1,0:T(8,128)S(1)} %get-tuple-element.967), channel_id=1, source_target_pairs={{0,1},{1,2},{2,3},{3,4},{4,5},{5,6},{6,7},{8,9},{9,10},{10,11},{11... | collective-permute-start | bytes 36872 | tf_op jit(solution)/shard_map/ppermute | solution.py:15
  391.6 24.5 %while.101 = (s32[]{:T(128)}, f32[32,256]{1,0:T(8,128)S(1)}, f32[65,65]{1,0:T(8,128)S(1)}, f32[96,320]{1,0:T(8,128)S(1)}, s32[]{:T(128)}, /*index=5*/s32[]{:T(12...) while((s32[]{:T(128)}, f32[32,256]{1,0:T(8,128)S(1)}, ...), condition=%wide.region_24.25_spmd.clone, body=%wide.region_23.24_spmd.clone.sunk | while | flops 47235088 | bytes 1324147 | solution.py:73
  418.7 10.8 %psum.101 = f32[4]{0:T(128)S(1)} all-reduce(f32[4]{0:T(128)S(1)} %convolution_bitcast_fusion), channel_id=1, replica_groups=mesh['gx'=4,'gy'=8] {'gy'}, use_global_device_ids=true, to_apply=%region_25.26 | all-reduce | flops 4 | bytes 32 | tf_op jit(solution)/shard_map/psum | solution.py:86
  430.9 6.2 %psum.102 = f32[4]{0:T(128)S(1)} all-reduce(f32[4]{0:T(128)S(1)} %psum.101), channel_id=1, replica_groups=mesh['gx'=4,'gy'=8] {'gx'}, use_global_device_ids=true, to_apply=%region_26.27 | all-reduce | flops 4 | bytes 32 | tf_op jit(solution)/shard_map/psum | solution.py:86
  438.2 42.8 %psum.103 = f32[]{:T(128)} all-reduce(f32[]{:T(128)} %fusion.60), channel_id=1, replica_groups=mesh['gx'=4,'gy'=8] {'gx','gy'}, use_global_device_ids=true, to_apply=%region_28.29 | all-reduce | flops 1 | bytes 8 | tf_op jit(solution)/shard_map/psum | solution.py:41
  512.2 7.4 %collective-permute-start.18 = (f32[96,32]{1,0:T(8,128)S(1)}, f32[96,32]{1,0:T(8,128)S(1)}, u32[]{:S(2)}, u32[]{:S(2)}) collective-permute-start(f32[96,32]{1,0:T(8,128)S(1)} %get-tuple-element.965), channel_id=1, source_target_pairs={{0,1},{1,2},{2,3},{3,4},{4,5},{5,6},{6,7},{8,9},{9,10},{10,11},{11... | collective-permute-start | bytes 36872 | tf_op jit(solution)/shard_map/ppermute | solution.py:15
  521.6 3.5 collective-permute-done.19
  525.1 24.5 %while.102 = (s32[]{:T(128)}, f32[32,256]{1,0:T(8,128)S(1)}, f32[65,65]{1,0:T(8,128)S(1)}, f32[96,320]{1,0:T(8,128)S(1)}, s32[]{:T(128)}, /*index=5*/s32[]{:T(12...) while((s32[]{:T(128)}, f32[32,256]{1,0:T(8,128)S(1)}, ...), condition=%wide.region_32.33_spmd.clone, body=%wide.region_31.32_spmd.clone.sunk | while | flops 47235088 | bytes 1324147 | solution.py:73
  (902 shorter events, 202.2 us)
Async XLA Ops:
  0.6 42.1 %copy-start.1 = (f32[32,256]{1,0:T(8,128)S(1)}, f32[32,256]{1,0:T(8,128)}, u32[]{:S(2)}) copy-start(f32[32,256]{1,0:T(8,128)} %param.29) | copy-start | bytes 98308
  42.7 5.3 copy-start.5
  42.7 6.6 %collective-permute-start = (f32[32,256]{1,0:T(8,128)S(1)}, f32[32,256]{1,0:T(8,128)S(1)}, u32[]{:S(2)}, u32[]{:S(2)}) collective-permute-start(f32[32,256]{1,0:T(8,128)S(1)} %broadcast_divide_fusion.3), channel_id=1, source_target_pairs={{0,8},{8,16},{16,24},{1,9},{9,17},{17,25},{2,10},{10,18},{18,26},{... | collective-permute-start | bytes 98312 | tf_op jit(solution)/shard_map/ppermute | solution.py:15
  45.9 5.6 %collective-permute-start.1 = (f32[32,256]{1,0:T(8,128)S(1)}, f32[32,256]{1,0:T(8,128)S(1)}, u32[]{:S(2)}, u32[]{:S(2)}) collective-permute-start(f32[32,256]{1,0:T(8,128)S(1)} %broadcast_divide_fusion.3), channel_id=1, source_target_pairs={{8,0},{16,8},{24,16},{9,1},{17,9},{25,17},{10,2},{18,10},{26,18},{... | collective-permute-start | bytes 98312 | tf_op jit(solution)/shard_map/ppermute | solution.py:18
  51.5 9.5 %collective-permute-start.2 = (f32[96,32]{1,0:T(8,128)S(1)}, f32[96,32]{1,0:T(8,128)S(1)}, u32[]{:S(2)}, u32[]{:S(2)}) collective-permute-start(f32[96,32]{1,0:T(8,128)S(1)} %get-tuple-element.973), channel_id=1, source_target_pairs={{0,1},{1,2},{2,3},{3,4},{4,5},{5,6},{6,7},{8,9},{9,10},{10,11},{11... | collective-permute-start | bytes 36872 | tf_op jit(solution)/shard_map/ppermute | solution.py:15
  58.3 5.4 collective-permute-start.3
  63.9 24.5 %copy-start.2 = (f32[32,256]{1,0:T(8,128)S(1)}, f32[32,256]{1,0:T(8,128)}, u32[]{:S(2)}) copy-start(f32[32,256]{1,0:T(8,128)} %param.30) | copy-start | bytes 98308
  151.9 5.3 collective-permute-start.4
  155.0 5.6 %collective-permute-start.5 = (f32[32,256]{1,0:T(8,128)S(1)}, f32[32,256]{1,0:T(8,128)S(1)}, u32[]{:S(2)}, u32[]{:S(2)}) collective-permute-start(f32[32,256]{1,0:T(8,128)S(1)} %broadcast_divide_fusion.2), channel_id=1, source_target_pairs={{8,0},{16,8},{24,16},{9,1},{17,9},{25,17},{10,2},{18,10},{26,18},{... | collective-permute-start | bytes 98312 | tf_op jit(solution)/shard_map/ppermute | solution.py:18
  160.7 9.2 %collective-permute-start.6 = (f32[96,32]{1,0:T(8,128)S(1)}, f32[96,32]{1,0:T(8,128)S(1)}, u32[]{:S(2)}, u32[]{:S(2)}) collective-permute-start(f32[96,32]{1,0:T(8,128)S(1)} %get-tuple-element.971), channel_id=1, source_target_pairs={{0,1},{1,2},{2,3},{3,4},{4,5},{5,6},{6,7},{8,9},{9,10},{10,11},{11... | collective-permute-start | bytes 36872 | tf_op jit(solution)/shard_map/ppermute | solution.py:15
  167.9 5.4 collective-permute-start.7
  260.5 5.9 %collective-permute-start.8 = (f32[32,256]{1,0:T(8,128)S(1)}, f32[32,256]{1,0:T(8,128)S(1)}, u32[]{:S(2)}, u32[]{:S(2)}) collective-permute-start(f32[32,256]{1,0:T(8,128)S(1)} %broadcast_divide_fusion.1), channel_id=1, source_target_pairs={{0,8},{8,16},{16,24},{1,9},{9,17},{17,25},{2,10},{10,18},{18,26},{... | collective-permute-start | bytes 98312 | tf_op jit(solution)/shard_map/ppermute | solution.py:15
  263.6 5.6 %collective-permute-start.9 = (f32[32,256]{1,0:T(8,128)S(1)}, f32[32,256]{1,0:T(8,128)S(1)}, u32[]{:S(2)}, u32[]{:S(2)}) collective-permute-start(f32[32,256]{1,0:T(8,128)S(1)} %broadcast_divide_fusion.1), channel_id=1, source_target_pairs={{8,0},{16,8},{24,16},{9,1},{17,9},{25,17},{10,2},{18,10},{26,18},{... | collective-permute-start | bytes 98312 | tf_op jit(solution)/shard_map/ppermute | solution.py:18
  269.3 9.2 %collective-permute-start.10 = (f32[96,32]{1,0:T(8,128)S(1)}, f32[96,32]{1,0:T(8,128)S(1)}, u32[]{:S(2)}, u32[]{:S(2)}) collective-permute-start(f32[96,32]{1,0:T(8,128)S(1)} %get-tuple-element.969), channel_id=1, source_target_pairs={{0,1},{1,2},{2,3},{3,4},{4,5},{5,6},{6,7},{8,9},{9,10},{10,11},{11... | collective-permute-start | bytes 36872 | tf_op jit(solution)/shard_map/ppermute | solution.py:15
  276.5 5.4 collective-permute-start.11
  370.0 8.8 %collective-permute-start.12 = (f32[32,256]{1,0:T(8,128)S(1)}, f32[32,256]{1,0:T(8,128)S(1)}, u32[]{:S(2)}, u32[]{:S(2)}) collective-permute-start(f32[32,256]{1,0:T(8,128)S(1)} %broadcast_divide_fusion), channel_id=1, source_target_pairs={{0,8},{8,16},{16,24},{1,9},{9,17},{17,25},{2,10},{10,18},{18,26},{... | collective-permute-start | bytes 98312 | tf_op jit(solution)/shard_map/ppermute | solution.py:15
  373.1 5.7 %collective-permute-start.13 = (f32[32,256]{1,0:T(8,128)S(1)}, f32[32,256]{1,0:T(8,128)S(1)}, u32[]{:S(2)}, u32[]{:S(2)}) collective-permute-start(f32[32,256]{1,0:T(8,128)S(1)} %broadcast_divide_fusion), channel_id=1, source_target_pairs={{8,0},{16,8},{24,16},{9,1},{17,9},{25,17},{10,2},{18,10},{26,18},{... | collective-permute-start | bytes 98312 | tf_op jit(solution)/shard_map/ppermute | solution.py:18
  378.9 9.1 %collective-permute-start.14 = (f32[96,32]{1,0:T(8,128)S(1)}, f32[96,32]{1,0:T(8,128)S(1)}, u32[]{:S(2)}, u32[]{:S(2)}) collective-permute-start(f32[96,32]{1,0:T(8,128)S(1)} %get-tuple-element.967), channel_id=1, source_target_pairs={{0,1},{1,2},{2,3},{3,4},{4,5},{5,6},{6,7},{8,9},{9,10},{10,11},{11... | collective-permute-start | bytes 36872 | tf_op jit(solution)/shard_map/ppermute | solution.py:15
  386.0 5.4 collective-permute-start.15
  503.4 46.2 %copy-start.3 = (f32[32,256]{1,0:T(8,128)}, f32[32,256]{1,0:T(8,128)S(1)}, u32[]{:S(2)}) copy-start(f32[32,256]{1,0:T(8,128)S(1)} %multiply_add_fusion) | copy-start | bytes 98308
  503.4 5.3 collective-permute-start.16
  506.5 5.6 %collective-permute-start.17 = (f32[32,256]{1,0:T(8,128)S(1)}, f32[32,256]{1,0:T(8,128)S(1)}, u32[]{:S(2)}, u32[]{:S(2)}) collective-permute-start(f32[32,256]{1,0:T(8,128)S(1)} %multiply_add_fusion), channel_id=1, source_target_pairs={{8,0},{16,8},{24,16},{9,1},{17,9},{25,17},{10,2},{18,10},{26,18},{... | collective-permute-start | bytes 98312 | tf_op jit(solution)/shard_map/ppermute | solution.py:18
  512.2 9.4 %collective-permute-start.18 = (f32[96,32]{1,0:T(8,128)S(1)}, f32[96,32]{1,0:T(8,128)S(1)}, u32[]{:S(2)}, u32[]{:S(2)}) collective-permute-start(f32[96,32]{1,0:T(8,128)S(1)} %get-tuple-element.965), channel_id=1, source_target_pairs={{0,1},{1,2},{2,3},{3,4},{4,5},{5,6},{6,7},{8,9},{9,10},{10,11},{11... | collective-permute-start | bytes 36872 | tf_op jit(solution)/shard_map/ppermute | solution.py:15
  519.6 5.4 collective-permute-start.19
  (2 other events, 3.6 us)
